TPU v7x, 128 devices: a whole 4x4x4 slice. The times are simulated.
128 devices in a mesh: chain: 64 (over z, x_hi, y, core), aux: 2 (over x_lo).
Axes of the slice: x: 4 (x_hi: 2, x_lo: 2; x = x_hi * 2 + x_lo), y: 4, z: 4, core: 2. Of those that a mesh axis runs over, the one named last changes fastest.
Arguments:
- occupied: bfloat16 [8192, 1152], P('chain'), may hold values from -0.1875 to 0.1875
- virtual: bfloat16 [8192, 1152], P('chain'), may hold values from -0.1875 to 0.1875
- three_centre: bfloat16 [32, 8192, 1152], P('aux', 'chain'), may hold values from -6 to 6
- kernel: bfloat16 [32, 32], P('aux'), may hold values from -1 to 1
- profile: int32 [64], replicated, may hold values from 2 to 4
- atom_map: int32 [32], P('aux'), may hold values from 0 to 63
Outputs:
- band_gradient: float32 [8192, 1152], P(('chain', 'aux'))
- polarization: float32 [32, 32], P('aux')
All inputs are finite; a program needn't handle non-finite values.
Results may differ from a plain program's by a relative error of at most 0.0042.
Values may be sent and summed in bfloat16 or wider, within the bound.
A program may use at most 128 MiB of HBM per device.

v0:
```python
import math
import jax
import jax.numpy as jnp
from jax import lax
from jax.sharding import PartitionSpec as P


def passed_along(block, axis, distance):
    devices = range(lax.axis_size(axis))
    route = [(i - distance, i) for i in devices if i - distance in devices]
    return lax.ppermute(block, axis, route)


def from_everyone(shard, axis):
    size = lax.axis_size(axis)
    return lax.all_to_all(
        jnp.broadcast_to(shard[None], (size, *shard.shape)), axis, 0, 0, tiled=True
    )


def taken_together(shard, axis):
    everything = from_everyone(shard, axis)
    return jnp.sum(everything, axis=0)


def cut_along(shard, dim, size):
    before, after = (shard.shape[:dim], shard.shape[dim + 1 :])
    return jnp.moveaxis(shard.reshape(*before, size, -1, *after), dim, 0)


def sent_and_summed(shard, axis, dim):
    parts = cut_along(shard, dim, lax.axis_size(axis))
    arrived = lax.all_to_all(parts, axis, split_axis=0, concat_axis=0, tiled=True)
    return arrived.sum(axis=0)


def shift_blocks(matrix, offset, block_size):
    if offset == 0:
        return matrix
    padding = jnp.zeros(matrix.shape[:-1] + (abs(offset) * block_size,), matrix.dtype)
    if offset > 0:
        return jnp.concatenate([padding, matrix[..., : -offset * block_size]], -1)
    return jnp.concatenate([matrix[..., -offset * block_size :], padding], -1)


def body(occupied, virtual, three_centre, kernel, profile, atom_map):
    block_size = occupied.shape[0]
    band_cols = occupied.shape[1]
    slots_total = band_cols // block_size
    spread = (slots_total - 1) // 2
    nblocks = lax.axis_size("chain")
    position = lax.axis_index("chain")
    slot_ids = jnp.arange(slots_total, dtype=jnp.int32)
    block_ids = jnp.arange(nblocks, dtype=jnp.int32)
    others = position + slot_ids - spread
    neighbours = jnp.sum(jnp.where(block_ids[None, :] == others[:, None], profile[None, :], 0), 1)
    own_width = jnp.sum(jnp.where(block_ids == position, profile, 0))
    allowed = jnp.abs(slot_ids - spread) <= jnp.minimum(own_width, neighbours)
    column_keep = jnp.repeat(allowed, block_size)
    zero_half = jnp.zeros((), jnp.bfloat16)
    occ_masked = jnp.where(column_keep[None, :], occupied, zero_half)
    vir_masked = jnp.where(column_keep[None, :], virtual, zero_half)
    both_bands = jnp.stack([occ_masked, vir_masked])
    fetched = []
    for slot_index in range(slots_total):
        if slot_index == spread:
            fetched.append(both_bands)
        else:
            fetched.append(passed_along(both_bands, "chain", spread - slot_index))
    stack_occ = jnp.concatenate(
        [shift_blocks(fetched[k][0], k - spread, block_size) for k in range(slots_total)], 0
    )
    stack_vir = jnp.concatenate(
        [shift_blocks(fetched[k][1], k - spread, block_size) for k in range(slots_total)], 0
    )
    aux_here = three_centre.shape[0]
    aux_total = kernel.shape[1]
    screen = jnp.abs(atom_map - position) <= nblocks // 4
    local = jnp.where(column_keep[None, None, :] & screen[:, None, None], three_centre, zero_half)
    screened = local.reshape(aux_here * block_size, band_cols)
    coupled = jnp.dot(screened, stack_occ, preferred_element_type=jnp.float32).astype(jnp.bfloat16)
    coupled = coupled.reshape(aux_here, block_size * band_cols)
    partner = jnp.dot(screened, stack_vir, preferred_element_type=jnp.float32).astype(jnp.bfloat16)
    partner = partner.reshape(aux_here, block_size, band_cols)
    piece = lax.all_gather(partner, "aux", axis=0, tiled=True)
    piece_rows = piece.shape[0]
    columns = piece.reshape(piece_rows, block_size * band_cols)
    products = lax.dot_general(
        coupled, columns, (((1,), (1,)), ((), ())), preferred_element_type=jnp.float32
    )
    polar_part = products
    response_sum = jnp.dot(kernel, columns, preferred_element_type=jnp.float32)
    polar_part, response_sum = (polar_part, response_sum)
    polarization = taken_together(polar_part, "chain") * (
        1.0 / math.sqrt(block_size * nblocks * band_cols)
    )
    response = response_sum.astype(jnp.bfloat16).reshape(aux_here * block_size, band_cols)
    partials = lax.dot_general(
        screened, response, (((0,), (0,)), ((), ())), preferred_element_type=jnp.float32
    )
    partials = partials.reshape(slots_total, block_size, band_cols)
    gathered_sum = partials[spread]
    for slot_index in range(slots_total):
        if slot_index != spread:
            moved = shift_blocks(partials[slot_index], spread - slot_index, block_size)
            gathered_sum = gathered_sum + passed_along(
                moved.astype(jnp.bfloat16), "chain", slot_index - spread
            ).astype(moved.dtype)
    gathered_sum = sent_and_summed(gathered_sum, "aux", 0)
    scale_grad = 1.0 / math.sqrt(block_size * aux_total)
    band_gradient = (
        jnp.where(column_keep[None, :], gathered_sum, jnp.zeros((), jnp.float32)) * scale_grad
    )
    return (band_gradient, polarization)


def solution(mesh):
    placed = (
        P("chain", None),
        P("chain", None),
        P("aux", "chain", None),
        P("aux", None),
        P(),
        P("aux"),
    )
    return jax.shard_map(
        body,
        mesh=mesh,
        in_specs=placed,
        out_specs=(P(("chain", "aux"), None), P("aux", None)),
        check_vma=False,
    )
```

profile of v0, /device:TPU:1, one launch (start us, length us, event | category | flops | bytes accessed | tf_op | source)
XLA Modules:
  0.0 339.7 jit_solution(14269273563489841605)
XLA Ops:
  7.2 1.3 fusion.12
  8.5 0.8 select_reduce_fusion
  10.1 1.1 fusion.9
  11.3 5.7 %collective-permute-start = (bf16[2,128,1152]{2,1,0:T(8,128)(2,1)S(1)}, bf16[2,128,1152]{2,1,0:T(8,128)(2,1)S(1)}, u32[]{:S(2)}, u32[]{:S(2)}) collective-permute-start(bf16[2,128,1152]{2,1,0:T(8,128)(2,1)S(1)} %pad_maximum_fusion), channel_id=1, source_target_pairs={{0,8},{2,10},{4,12},{6,14},{8,16},{10,18},{12,20},{14,22},{16,24},... | collective-permute-start | bytes 1769480 | tf_op jit(solution)/shard_map/ppermute | solution.py:11
  17.0 5.3 %collective-permute-start.1 = (bf16[2,128,1152]{2,1,0:T(8,128)(2,1)S(1)}, bf16[2,128,1152]{2,1,0:T(8,128)(2,1)S(1)}, u32[]{:S(2)}, u32[]{:S(2)}) collective-permute-start(bf16[2,128,1152]{2,1,0:T(8,128)(2,1)S(1)} %pad_maximum_fusion), channel_id=1, source_target_pairs={{0,6},{2,8},{4,10},{6,12},{8,14},{10,16},{12,18},{14,20},{16,22},{... | collective-permute-start | bytes 1769480 | tf_op jit(solution)/shard_map/ppermute | solution.py:11
  22.2 3.2 collective-permute-start.2
  25.5 1.9 collective-permute-start.3
  27.4 2.4 collective-permute-start.4
  30.6 2.8 broadcast_select_fusion
  33.4 1.3 collective-permute-start.5
  34.8 6.8 %collective-permute-done.1 = bf16[2,128,1152]{2,1,0:T(8,128)(2,1)S(1)} collective-permute-done((bf16[2,128,1152]{2,1,0:T(8,128)(2,1)S(1)}, bf16[2,128,1152]{2,1,0:T(8,128)(2,1)S(1)}, u32[]{:S(2)}, u32[]{:S(2)}) %collective-permute-start.1) | collective-permute-done | bytes 589856 | tf_op jit(solution)/shard_map/ppermute | solution.py:11
  41.6 1.3 collective-permute-start.6
  43.0 11.3 %collective-permute-done.2 = bf16[2,128,1152]{2,1,0:T(8,128)(2,1)S(1)} collective-permute-done((bf16[2,128,1152]{2,1,0:T(8,128)(2,1)S(1)}, bf16[2,128,1152]{2,1,0:T(8,128)(2,1)S(1)}, u32[]{:S(2)}, u32[]{:S(2)}) %collective-permute-start.2) | collective-permute-done | bytes 589856 | tf_op jit(solution)/shard_map/ppermute | solution.py:11
  54.3 1.3 collective-permute-start.7
  55.6 8.8 %collective-permute-done.3 = bf16[2,128,1152]{2,1,0:T(8,128)(2,1)S(1)} collective-permute-done((bf16[2,128,1152]{2,1,0:T(8,128)(2,1)S(1)}, bf16[2,128,1152]{2,1,0:T(8,128)(2,1)S(1)}, u32[]{:S(2)}, u32[]{:S(2)}) %collective-permute-start.3) | collective-permute-done | bytes 589856 | tf_op jit(solution)/shard_map/ppermute | solution.py:11
  64.5 14.6 %collective-permute-done.6 = bf16[2,128,1152]{2,1,0:T(8,128)(2,1)S(1)} collective-permute-done((bf16[2,128,1152]{2,1,0:T(8,128)(2,1)S(1)}, bf16[2,128,1152]{2,1,0:T(8,128)(2,1)S(1)}, u32[]{:S(2)}, u32[]{:S(2)}) %collective-permute-start.6) | collective-permute-done | bytes 589856 | tf_op jit(solution)/shard_map/ppermute | solution.py:11
  81.0 8.5 %convolution_convert_fusion.2 = bf16[2048,1152]{1,0:T(8,128)(2,1)} fusion(bf16[2048,1152]{1,0:T(8,128)(2,1)S(1)} %bitcast.61, bf16[1152,1152]{1,0:T(8,128)(2,1)S(1)} %pad_dynamic-update-slice_fusion.8), kind=kOutput, calls=%fused_computation.3 | convolution fusion | flops 5438177280 | bytes 12091392 | tf_op jit(solution)/shard_map/dot_general | solution.py:83
  89.6 0.7 pad_dynamic-update-slice_fusion.2
  90.4 0.7 pad_dynamic-update-slice_fusion.1
  91.8 10.9 %convolution_convert_fusion.1 = bf16[2048,1152]{1,0:T(8,128)(2,1)} fusion(bf16[2048,1152]{1,0:T(8,128)(2,1)} %bitcast.62, bf16[1152,1152]{1,0:T(8,128)(2,1)} %pad_dynamic-update-slice_fusion), kind=kOutput, calls=%fused_computation.2 | convolution fusion | flops 5438177280 | bytes 12091392 | tf_op jit(solution)/shard_map/dot_general | solution.py:81
  102.7 5.2 %reshape.85 = bf16[16,147456]{1,0:T(8,128)(2,1)} reshape(bf16[2048,1152]{1,0:T(8,128)(2,1)} %convolution_convert_fusion.1) | data formatting | bytes 9437184 | tf_op jit(solution)/shard_map/reshape | solution.py:82
  107.9 110.5 %all-gather.2.cloned.1.call-done = bf16[32,128,1152]{2,1,0:T(8,128)(2,1)} async-done(((bf16[16,128,1152]{2,1,0:T(8,128)(2,1)}), bf16[32,128,1152]{2,1,0:T(8,128)(2,1)}) %all-gather.2.cloned.1.call-update) | async-done | bytes 9437200 | tf_op jit(solution)/shard_map/all_gather | solution.py:85
  218.4 12.7 %copy.10 = bf16[4,8,128,1152]{3,1,2,0:T(8,128)(2,1)} copy(bf16[4,8,128,1152]{3,2,1,0:T(8,128)(2,1)} %bitcast.59) | data formatting | bytes 18874368
  231.2 7.2 %fusion = bf16[16,147456]{1,0:T(8,128)(2,1)} fusion(bf16[16,32]{1,0:T(8,128)(2,1)S(1)} %copy-done, bf16[32,147456]{1,0:T(8,128)(2,1)} %bitcast.55), kind=kOutput, calls=%fused_computation.1 | convolution fusion | flops 153354240 | bytes 14156800 | tf_op jit(solution)/shard_map/dot_general | solution.py:92
  238.4 5.3 %reshape.83 = bf16[2048,1152]{1,0:T(8,128)(2,1)} reshape(bf16[16,147456]{1,0:T(8,128)(2,1)} %fusion) | data formatting | bytes 9437184 | tf_op jit(solution)/shard_map/reshape | solution.py:97
  243.7 12.6 %fusion.17 = (bf16[1152,1152]{1,0:T(8,128)(2,1)S(1)}, f32[1152,1152]{1,0:T(8,128)}) fusion(bf16[2048,1152]{1,0:T(8,128)(2,1)} %bitcast.63, bf16[2048,1152]{1,0:T(8,128)(2,1)} %reshape.83), kind=kOutput, calls=%fused_computation.67 | convolution fusion | flops 5437145088 | bytes 17399808 | tf_op jit(solution)/shard_map/dot_general | solution.py:98
  256.4 2.7 collective-permute-start.11
  259.2 3.0 collective-permute-start.12
  262.3 1.3 collective-permute-start.10
  263.6 0.7 concatenate.92
  264.3 4.0 %collective-permute-start.13 = (bf16[128,1152]{1,0:T(8,128)(2,1)}, bf16[128,1152]{1,0:T(8,128)(2,1)S(1)}, u32[]{:S(2)}, u32[]{:S(2)}) collective-permute-start(bf16[128,1152]{1,0:T(8,128)(2,1)} %concatenate.92), channel_id=1, source_target_pairs={{0,4},{2,6},{4,8},{6,10},{8,12},{10,14},{12,16},{14,18},{16,20},{1... | collective-permute-start | bytes 884744 | tf_op jit(solution)/shard_map/ppermute | solution.py:11
  268.3 0.7 concatenate.93
  269.1 4.5 %collective-permute-start.14 = (bf16[128,1152]{1,0:T(8,128)(2,1)}, bf16[128,1152]{1,0:T(8,128)(2,1)S(1)}, u32[]{:S(2)}, u32[]{:S(2)}) collective-permute-start(bf16[128,1152]{1,0:T(8,128)(2,1)} %concatenate.93), channel_id=1, source_target_pairs={{0,6},{2,8},{4,10},{6,12},{8,14},{10,16},{12,18},{14,20},{16,22},{... | collective-permute-start | bytes 884744 | tf_op jit(solution)/shard_map/ppermute | solution.py:11
  273.5 0.7 concatenate.88
  274.3 0.7 concatenate.94
  275.0 0.7 concatenate.87
  275.8 1.3 collective-permute-start.9
  277.1 7.3 %collective-permute-start.15 = (bf16[128,1152]{1,0:T(8,128)(2,1)}, bf16[128,1152]{1,0:T(8,128)(2,1)S(1)}, u32[]{:S(2)}, u32[]{:S(2)}) collective-permute-start(bf16[128,1152]{1,0:T(8,128)(2,1)} %concatenate.94), channel_id=1, source_target_pairs={{0,8},{2,10},{4,12},{6,14},{8,16},{10,18},{12,20},{14,22},{16,24},... | collective-permute-start | bytes 884744 | tf_op jit(solution)/shard_map/ppermute | solution.py:11
  284.4 1.3 collective-permute-start.8
  285.8 4.3 %fusion.18 = f32[16,32]{1,0:T(8,128)S(1)} fusion(bf16[16,147456]{1,0:T(8,128)(2,1)} %reshape.85, bf16[32,147456]{1,0:T(8,128)(2,1)S(1)} %bitcast.58), kind=kOutput, calls=%fused_computation.68 | convolution fusion | flops 150994944 | bytes 14157824 | tf_op jit(solution)/shard_map/dot_general | solution.py:88
  290.2 0.9 reshape.86
  291.1 19.2 %all-to-all-start.1 = ((f32[64,1,512]{2,1,0:T(1,128)}), f32[64,1,512]{2,1,0:T(1,128)S(1)}, u32[]{:S(2)}, u32[]{:S(2)}) async-start(f32[64,1,512]{2,1,0:T(1,128)} %reshape.86), calls=%async_computation.1 | async-start | bytes 262144 | tf_op jit(solution)/shard_map/all_to_all | solution.py:16
  310.3 2.2 fusion.7
  312.5 7.8 %all-to-all-done.1 = f32[64,1,512]{2,1,0:T(1,128)S(1)} async-done(((f32[64,1,512]{2,1,0:T(1,128)}), f32[64,1,512]{2,1,0:T(1,128)S(1)}, u32[]{:S(2)}, u32[]{:S(2)}) %all-to-all-start.1) | async-done | bytes 131104 | tf_op jit(solution)/shard_map/all_to_all | solution.py:16
  320.2 3.5 %all-to-all-start = ((f32[2,64,1152]{2,1,0:T(8,128)}), f32[2,64,1152]{2,1,0:T(8,128)S(1)}, u32[]{:S(2)}, u32[]{:S(2)}) async-start(f32[2,64,1152]{2,1,0:T(8,128)} %bitcast.14), calls=%async_computation | async-start | bytes 1179648 | tf_op jit(solution)/shard_map/all_to_all | solution.py:33
  324.3 1.0 reduce
  326.1 6.0 %all-to-all-done = f32[2,64,1152]{2,1,0:T(8,128)S(1)} async-done(((f32[2,64,1152]{2,1,0:T(8,128)}), f32[2,64,1152]{2,1,0:T(8,128)S(1)}, u32[]{:S(2)}, u32[]{:S(2)}) %all-to-all-start) | async-done | bytes 589856 | tf_op jit(solution)/shard_map/all_to_all | solution.py:33
  332.1 0.7 select_multiply_fusion
  (88 shorter events, 5.9 us)
Async XLA Ops:
  7.2 224.0 %copy-start = (bf16[16,32]{1,0:T(8,128)(2,1)S(1)}, bf16[16,32]{1,0:T(8,128)(2,1)}, u32[]{:S(2)}) copy-start(bf16[16,32]{1,0:T(8,128)(2,1)} %param.9) | copy-start | bytes 3076
  7.2 211.3 %all-gather.2.cloned.1.call-start = ((), (), s32[]{:S(2)}) async-start(), calls=%async_computation.2 | async-start | bytes 14155776 | tf_op jit(solution)/shard_map/all_gather | solution.py:85
  11.3 22.1 %collective-permute-start = (bf16[2,128,1152]{2,1,0:T(8,128)(2,1)S(1)}, bf16[2,128,1152]{2,1,0:T(8,128)(2,1)S(1)}, u32[]{:S(2)}, u32[]{:S(2)}) collective-permute-start(bf16[2,128,1152]{2,1,0:T(8,128)(2,1)S(1)} %pad_maximum_fusion), channel_id=1, source_target_pairs={{0,8},{2,10},{4,12},{6,14},{8,16},{10,18},{12,20},{14,22},{16,24},... | collective-permute-start | bytes 1769480 | tf_op jit(solution)/shard_map/ppermute | solution.py:11
  17.0 24.6 %collective-permute-start.1 = (bf16[2,128,1152]{2,1,0:T(8,128)(2,1)S(1)}, bf16[2,128,1152]{2,1,0:T(8,128)(2,1)S(1)}, u32[]{:S(2)}, u32[]{:S(2)}) collective-permute-start(bf16[2,128,1152]{2,1,0:T(8,128)(2,1)S(1)} %pad_maximum_fusion), channel_id=1, source_target_pairs={{0,6},{2,8},{4,10},{6,12},{8,14},{10,16},{12,18},{14,20},{16,22},{... | collective-permute-start | bytes 1769480 | tf_op jit(solution)/shard_map/ppermute | solution.py:11
  22.2 32.0 %collective-permute-start.2 = (bf16[2,128,1152]{2,1,0:T(8,128)(2,1)S(1)}, bf16[2,128,1152]{2,1,0:T(8,128)(2,1)S(1)}, u32[]{:S(2)}, u32[]{:S(2)}) collective-permute-start(bf16[2,128,1152]{2,1,0:T(8,128)(2,1)S(1)} %pad_maximum_fusion), channel_id=1, source_target_pairs={{0,4},{2,6},{4,8},{6,10},{8,12},{10,14},{12,16},{14,18},{16,20},{1... | collective-permute-start | bytes 1769480 | tf_op jit(solution)/shard_map/ppermute | solution.py:11
  25.5 38.9 %collective-permute-start.3 = (bf16[2,128,1152]{2,1,0:T(8,128)(2,1)S(1)}, bf16[2,128,1152]{2,1,0:T(8,128)(2,1)S(1)}, u32[]{:S(2)}, u32[]{:S(2)}) collective-permute-start(bf16[2,128,1152]{2,1,0:T(8,128)(2,1)S(1)} %pad_maximum_fusion), channel_id=1, source_target_pairs={{0,2},{2,4},{4,6},{6,8},{8,10},{10,12},{12,14},{14,16},{16,18},{18... | collective-permute-start | bytes 1769480 | tf_op jit(solution)/shard_map/ppermute | solution.py:11
  27.4 37.0 %collective-permute-start.4 = (bf16[2,128,1152]{2,1,0:T(8,128)(2,1)S(1)}, bf16[2,128,1152]{2,1,0:T(8,128)(2,1)S(1)}, u32[]{:S(2)}, u32[]{:S(2)}) collective-permute-start(bf16[2,128,1152]{2,1,0:T(8,128)(2,1)S(1)} %pad_maximum_fusion), channel_id=1, source_target_pairs={{2,0},{4,2},{6,4},{8,6},{10,8},{12,10},{14,12},{16,14},{18,16},{20... | collective-permute-start | bytes 1769480 | tf_op jit(solution)/shard_map/ppermute | solution.py:11
  33.4 47.6 %copy-start.1 = (bf16[16,128,1152]{2,1,0:T(8,128)(2,1)}, bf16[16,128,1152]{2,1,0:T(8,128)(2,1)S(1)}, u32[]{:S(2)}) copy-start(bf16[16,128,1152]{2,1,0:T(8,128)(2,1)S(1)} %broadcast_select_fusion) | copy-start | bytes 14155780
  33.4 31.0 %collective-permute-start.5 = (bf16[2,128,1152]{2,1,0:T(8,128)(2,1)S(1)}, bf16[2,128,1152]{2,1,0:T(8,128)(2,1)S(1)}, u32[]{:S(2)}, u32[]{:S(2)}) collective-permute-start(bf16[2,128,1152]{2,1,0:T(8,128)(2,1)S(1)} %pad_maximum_fusion), channel_id=1, source_target_pairs={{4,0},{6,2},{8,4},{10,6},{12,8},{14,10},{16,12},{18,14},{20,16},{2... | collective-permute-start | bytes 1769480 | tf_op jit(solution)/shard_map/ppermute | solution.py:11
  41.6 37.6 %collective-permute-start.6 = (bf16[2,128,1152]{2,1,0:T(8,128)(2,1)S(1)}, bf16[2,128,1152]{2,1,0:T(8,128)(2,1)S(1)}, u32[]{:S(2)}, u32[]{:S(2)}) collective-permute-start(bf16[2,128,1152]{2,1,0:T(8,128)(2,1)S(1)} %pad_maximum_fusion), channel_id=1, source_target_pairs={{6,0},{8,2},{10,4},{12,6},{14,8},{16,10},{18,12},{20,14},{22,16},{... | collective-permute-start | bytes 1769480 | tf_op jit(solution)/shard_map/ppermute | solution.py:11
  54.3 25.4 %collective-permute-start.7 = (bf16[2,128,1152]{2,1,0:T(8,128)(2,1)S(1)}, bf16[2,128,1152]{2,1,0:T(8,128)(2,1)S(1)}, u32[]{:S(2)}, u32[]{:S(2)}) collective-permute-start(bf16[2,128,1152]{2,1,0:T(8,128)(2,1)S(1)} %pad_maximum_fusion), channel_id=1, source_target_pairs={{8,0},{10,2},{12,4},{14,6},{16,8},{18,10},{20,12},{22,14},{24,16},... | collective-permute-start | bytes 1769480 | tf_op jit(solution)/shard_map/ppermute | solution.py:11
  79.6 1.0 copy-start.2
  79.6 1.0 copy-start.3
  80.9 8.7 %copy-start.4 = (bf16[1152,1152]{1,0:T(8,128)(2,1)}, bf16[1152,1152]{1,0:T(8,128)(2,1)S(1)}, u32[]{:S(2)}) copy-start(bf16[1152,1152]{1,0:T(8,128)(2,1)S(1)} %get-tuple-element.32) | copy-start | bytes 7962628
  238.4 47.3 %slice-start = ((s8[9437184]{0:T(1024)(128)(4,1)}), s8[1048576]{0:T(1024)(128)(4,1)S(1)}, s32[]{:S(2)}) async-start(s8[9437184]{0:T(1024)(128)(4,1)} %bitcast.56), calls=%async_computation.3 | async-start | bytes 2097152
  243.7 42.1 %slice-start.1 = ((s8[9437184]{0:T(1024)(128)(4,1)}), s8[4194304]{0:T(1024)(128)(4,1)S(1)}, s32[]{:S(2)}) async-start(s8[9437184]{0:T(1024)(128)(4,1)} %bitcast.56), calls=%async_computation.4 | async-start | bytes 8388608
  243.7 42.1 %slice-start.2 = ((s8[9437184]{0:T(1024)(128)(4,1)}), s8[4194304]{0:T(1024)(128)(4,1)S(1)}, s32[]{:S(2)}) async-start(s8[9437184]{0:T(1024)(128)(4,1)} %bitcast.56), calls=%async_computation.5 | async-start | bytes 8388608
  256.4 19.4 %collective-permute-start.11 = (bf16[128,1152]{1,0:T(8,128)(2,1)S(1)}, bf16[128,1152]{1,0:T(8,128)(2,1)S(1)}, u32[]{:S(2)}, u32[]{:S(2)}) collective-permute-start(bf16[128,1152]{1,0:T(8,128)(2,1)S(1)} %concatenate.90), channel_id=1, source_target_pairs={{2,0},{4,2},{6,4},{8,6},{10,8},{12,10},{14,12},{16,14},{18,16},{20... | collective-permute-start | bytes 884744 | tf_op jit(solution)/shard_map/ppermute | solution.py:11
  259.2 17.9 %collective-permute-start.12 = (bf16[128,1152]{1,0:T(8,128)(2,1)S(1)}, bf16[128,1152]{1,0:T(8,128)(2,1)S(1)}, u32[]{:S(2)}, u32[]{:S(2)}) collective-permute-start(bf16[128,1152]{1,0:T(8,128)(2,1)S(1)} %concatenate.91), channel_id=1, source_target_pairs={{0,2},{2,4},{4,6},{6,8},{8,10},{10,12},{12,14},{14,16},{16,18},{18... | collective-permute-start | bytes 884744 | tf_op jit(solution)/shard_map/ppermute | solution.py:11
  262.3 22.2 %collective-permute-start.10 = (bf16[128,1152]{1,0:T(8,128)(2,1)S(1)}, bf16[128,1152]{1,0:T(8,128)(2,1)S(1)}, u32[]{:S(2)}, u32[]{:S(2)}) collective-permute-start(bf16[128,1152]{1,0:T(8,128)(2,1)S(1)} %concatenate.89), channel_id=1, source_target_pairs={{4,0},{6,2},{8,4},{10,6},{12,8},{14,10},{16,12},{18,14},{20,16},{2... | collective-permute-start | bytes 884744 | tf_op jit(solution)/shard_map/ppermute | solution.py:11
  264.3 45.9 %collective-permute-start.13 = (bf16[128,1152]{1,0:T(8,128)(2,1)}, bf16[128,1152]{1,0:T(8,128)(2,1)S(1)}, u32[]{:S(2)}, u32[]{:S(2)}) collective-permute-start(bf16[128,1152]{1,0:T(8,128)(2,1)} %concatenate.92), channel_id=1, source_target_pairs={{0,4},{2,6},{4,8},{6,10},{8,12},{10,14},{12,16},{14,18},{16,20},{1... | collective-permute-start | bytes 884744 | tf_op jit(solution)/shard_map/ppermute | solution.py:11
  269.1 41.2 %collective-permute-start.14 = (bf16[128,1152]{1,0:T(8,128)(2,1)}, bf16[128,1152]{1,0:T(8,128)(2,1)S(1)}, u32[]{:S(2)}, u32[]{:S(2)}) collective-permute-start(bf16[128,1152]{1,0:T(8,128)(2,1)} %concatenate.93), channel_id=1, source_target_pairs={{0,6},{2,8},{4,10},{6,12},{8,14},{10,16},{12,18},{14,20},{16,22},{... | collective-permute-start | bytes 884744 | tf_op jit(solution)/shard_map/ppermute | solution.py:11
  275.8 34.5 %collective-permute-start.9 = (bf16[128,1152]{1,0:T(8,128)(2,1)}, bf16[128,1152]{1,0:T(8,128)(2,1)S(1)}, u32[]{:S(2)}, u32[]{:S(2)}) collective-permute-start(bf16[128,1152]{1,0:T(8,128)(2,1)} %concatenate.88), channel_id=1, source_target_pairs={{6,0},{8,2},{10,4},{12,6},{14,8},{16,10},{18,12},{20,14},{22,16},{... | collective-permute-start | bytes 884744 | tf_op jit(solution)/shard_map/ppermute | solution.py:11
  277.1 33.2 %collective-permute-start.15 = (bf16[128,1152]{1,0:T(8,128)(2,1)}, bf16[128,1152]{1,0:T(8,128)(2,1)S(1)}, u32[]{:S(2)}, u32[]{:S(2)}) collective-permute-start(bf16[128,1152]{1,0:T(8,128)(2,1)} %concatenate.94), channel_id=1, source_target_pairs={{0,8},{2,10},{4,12},{6,14},{8,16},{10,18},{12,20},{14,22},{16,24},... | collective-permute-start | bytes 884744 | tf_op jit(solution)/shard_map/ppermute | solution.py:11
  284.4 25.9 %collective-permute-start.8 = (bf16[128,1152]{1,0:T(8,128)(2,1)}, bf16[128,1152]{1,0:T(8,128)(2,1)S(1)}, u32[]{:S(2)}, u32[]{:S(2)}) collective-permute-start(bf16[128,1152]{1,0:T(8,128)(2,1)} %concatenate.87), channel_id=1, source_target_pairs={{8,0},{10,2},{12,4},{14,6},{16,8},{18,10},{20,12},{22,14},{24,16},... | collective-permute-start | bytes 884744 | tf_op jit(solution)/shard_map/ppermute | solution.py:11
  291.1 29.2 %all-to-all-start.1 = ((f32[64,1,512]{2,1,0:T(1,128)}), f32[64,1,512]{2,1,0:T(1,128)S(1)}, u32[]{:S(2)}, u32[]{:S(2)}) async-start(f32[64,1,512]{2,1,0:T(1,128)} %reshape.86), calls=%async_computation.1 | async-start | bytes 262144 | tf_op jit(solution)/shard_map/all_to_all | solution.py:16
  320.2 11.9 %all-to-all-start = ((f32[2,64,1152]{2,1,0:T(8,128)}), f32[2,64,1152]{2,1,0:T(8,128)S(1)}, u32[]{:S(2)}, u32[]{:S(2)}) async-start(f32[2,64,1152]{2,1,0:T(8,128)} %bitcast.14), calls=%async_computation | async-start | bytes 1179648 | tf_op jit(solution)/shard_map/all_to_all | solution.py:33
Sparse Core Ops, SparseCore 0:
  89.7 128.7 all-gather.1
where the time goes:
time: 341 us; the launch traced here: 340 us
  waiting for transfers between devices  166 us (49%)
  starting transfers between devices  70.5 us (21%)
  matrix products  43.6 us (13%)
  local copies, waits for them, and re-layouts  32.8 us (10%)
  between operations  14.7 us (4%)
  other arithmetic  12.3 us (4%)
    all_gather x1, waiting for transfers between devices, body(): piece = lax.all_gather(partner, 'aux', axis=0, tiled=True)  111 us
    ppermute x16, starting transfers between devices, passed_along(): return lax.ppermute(block, axis, route)  47.8 us
    ppermute x16, waiting for transfers between devices, passed_along(): return lax.ppermute(block, axis, route)  41.6 us
    all_to_all x1, starting transfers between devices, from_everyone(): lax.all_to_all(jnp.broadcast_to(shard[None], (size, *shard.shape)), axis,...  19.2 us
    unnamed x32, local copies, waits for them, and re-layouts  16.4 us
    dot_general x1, matrix products, body(): lax.dot_general(screened, response, (((0,), (0,)), ((), ())), preferred_e...  12.6 us
    dot_general x1, matrix products, body(): jnp.dot(screened, stack_occ, preferred_element_type=jnp.float32)  10.9 us
    dot_general x1, matrix products, body(): jnp.dot(screened, stack_vir, preferred_element_type=jnp.float32)  8.54 us
  transfers between devices with their start and end apart: 19, of which 7 were waited for; matrix products, arithmetic and copies ran while one was open for 11% of the time, Pallas kernels for 0%

commit v1 on v0

--- a/solution.py
+++ b/solution.py
@@ -82,7 +82,9 @@
     coupled = coupled.reshape(aux_here, block_size * band_cols)
     partner = jnp.dot(screened, stack_vir, preferred_element_type=jnp.float32).astype(jnp.bfloat16)
     partner = partner.reshape(aux_here, block_size, band_cols)
-    piece = lax.all_gather(partner, "aux", axis=0, tiled=True)
+    piece = jnp.concatenate(
+        lax.all_to_all(jnp.stack([partner] * lax.axis_size("aux")), "aux", 0, 0), axis=0
+    )
     piece_rows = piece.shape[0]
     columns = piece.reshape(piece_rows, block_size * band_cols)
     products = lax.dot_general(

time: 341 us -> 317 us (0.930)
  waiting for transfers between devices: 166 us -> 135 us
  between operations: 14.7 us -> 1.35 us
  starting transfers between devices: 70.5 us -> 82 us
  other arithmetic: 12.3 us -> 20.6 us
    all_gather x1 -> x0, waiting for transfers between devices: 111 us -> none  [body(): piece = lax.all_gather(partner, 'aux', axis=0, tiled=True)]
    all_to_all x0 -> x1, waiting for transfers between devices: none -> 80.1 us  [body(): lax.all_to_all(jnp.stack([partner] * lax.axis_size('aux')), 'aux', 0, 0)]
    another operation x0 -> x1, other arithmetic: none -> 8.33 us  [body(): jnp.stack([partner] * lax.axis_size('aux'))]
    all_to_all x0 -> x1, starting transfers between devices: none -> 7.32 us  [body(): lax.all_to_all(jnp.stack([partner] * lax.axis_size('aux')), 'aux', 0, 0)]
    ppermute x16, starting transfers between devices: 47.8 us -> 51.8 us  [passed_along(): return lax.ppermute(block, axis, route)]
where the time goes in v1:
time: 317 us; the launch traced here: 316 us
  waiting for transfers between devices  135 us (43%)
  starting transfers between devices  82 us (26%)
  matrix products  43.6 us (14%)
  local copies, waits for them, and re-layouts  32.8 us (10%)
  other arithmetic  20.6 us (6%)
    all_to_all x1, waiting for transfers between devices, body(): lax.all_to_all(jnp.stack([partner] * lax.axis_size('aux')), 'aux', 0, 0)  80.1 us
    ppermute x16, starting transfers between devices, passed_along(): return lax.ppermute(block, axis, route)  51.8 us
    ppermute x16, waiting for transfers between devices, passed_along(): return lax.ppermute(block, axis, route)  41.6 us
    all_to_all x1, starting transfers between devices, from_everyone(): lax.all_to_all(jnp.broadcast_to(shard[None], (size, *shard.shape)), axis,...  19.4 us
    unnamed x32, local copies, waits for them, and re-layouts  16.4 us
    dot_general x1, matrix products, body(): lax.dot_general(screened, response, (((0,), (0,)), ((), ())), preferred_e...  12.6 us
    dot_general x1, matrix products, body(): jnp.dot(screened, stack_occ, preferred_element_type=jnp.float32)  10.9 us
    dot_general x1, matrix products, body(): jnp.dot(screened, stack_vir, preferred_element_type=jnp.float32)  8.55 us
  transfers between devices with their start and end apart: 19, of which 7 were waited for; matrix products, arithmetic and copies ran while one was open for 11% of the time, Pallas kernels for 0%

profile of v1, /device:TPU:1, one launch (start us, length us, event | category | flops | bytes accessed | tf_op | source)
XLA Modules:
  0.0 315.8 jit_solution(3701856207009872673)
XLA Ops:
  0.7 1.3 fusion.12
  2.0 0.8 select_reduce_fusion
  3.5 1.1 fusion.9
  4.7 5.7 %collective-permute-start = (bf16[2,128,1152]{2,1,0:T(8,128)(2,1)S(1)}, bf16[2,128,1152]{2,1,0:T(8,128)(2,1)S(1)}, u32[]{:S(2)}, u32[]{:S(2)}) collective-permute-start(bf16[2,128,1152]{2,1,0:T(8,128)(2,1)S(1)} %pad_maximum_fusion.1), channel_id=1, source_target_pairs={{0,8},{2,10},{4,12},{6,14},{8,16},{10,18},{12,20},{14,22},{16,24},... | collective-permute-start | bytes 1769480 | tf_op jit(solution)/shard_map/ppermute | solution.py:11
  10.4 5.3 %collective-permute-start.1 = (bf16[2,128,1152]{2,1,0:T(8,128)(2,1)S(1)}, bf16[2,128,1152]{2,1,0:T(8,128)(2,1)S(1)}, u32[]{:S(2)}, u32[]{:S(2)}) collective-permute-start(bf16[2,128,1152]{2,1,0:T(8,128)(2,1)S(1)} %pad_maximum_fusion.1), channel_id=1, source_target_pairs={{0,6},{2,8},{4,10},{6,12},{8,14},{10,16},{12,18},{14,20},{16,22},{... | collective-permute-start | bytes 1769480 | tf_op jit(solution)/shard_map/ppermute | solution.py:11
  15.7 3.2 %collective-permute-start.2 = (bf16[2,128,1152]{2,1,0:T(8,128)(2,1)S(1)}, bf16[2,128,1152]{2,1,0:T(8,128)(2,1)S(1)}, u32[]{:S(2)}, u32[]{:S(2)}) collective-permute-start(bf16[2,128,1152]{2,1,0:T(8,128)(2,1)S(1)} %pad_maximum_fusion.1), channel_id=1, source_target_pairs={{0,4},{2,6},{4,8},{6,10},{8,12},{10,14},{12,16},{14,18},{16,20},{1... | collective-permute-start | bytes 1769480 | tf_op jit(solution)/shard_map/ppermute | solution.py:11
  18.9 1.9 collective-permute-start.3
  20.8 2.4 collective-permute-start.4
  24.0 2.8 broadcast_select_fusion
  26.9 1.3 collective-permute-start.5
  28.2 6.8 %collective-permute-done.1 = bf16[2,128,1152]{2,1,0:T(8,128)(2,1)S(1)} collective-permute-done((bf16[2,128,1152]{2,1,0:T(8,128)(2,1)S(1)}, bf16[2,128,1152]{2,1,0:T(8,128)(2,1)S(1)}, u32[]{:S(2)}, u32[]{:S(2)}) %collective-permute-start.1) | collective-permute-done | bytes 589856 | tf_op jit(solution)/shard_map/ppermute | solution.py:11
  35.0 1.3 collective-permute-start.6
  36.4 11.3 %collective-permute-done.2 = bf16[2,128,1152]{2,1,0:T(8,128)(2,1)S(1)} collective-permute-done((bf16[2,128,1152]{2,1,0:T(8,128)(2,1)S(1)}, bf16[2,128,1152]{2,1,0:T(8,128)(2,1)S(1)}, u32[]{:S(2)}, u32[]{:S(2)}) %collective-permute-start.2) | collective-permute-done | bytes 589856 | tf_op jit(solution)/shard_map/ppermute | solution.py:11
  47.7 1.3 collective-permute-start.7
  49.0 8.8 %collective-permute-done.3 = bf16[2,128,1152]{2,1,0:T(8,128)(2,1)S(1)} collective-permute-done((bf16[2,128,1152]{2,1,0:T(8,128)(2,1)S(1)}, bf16[2,128,1152]{2,1,0:T(8,128)(2,1)S(1)}, u32[]{:S(2)}, u32[]{:S(2)}) %collective-permute-start.3) | collective-permute-done | bytes 589856 | tf_op jit(solution)/shard_map/ppermute | solution.py:11
  58.0 14.6 %collective-permute-done.6 = bf16[2,128,1152]{2,1,0:T(8,128)(2,1)S(1)} collective-permute-done((bf16[2,128,1152]{2,1,0:T(8,128)(2,1)S(1)}, bf16[2,128,1152]{2,1,0:T(8,128)(2,1)S(1)}, u32[]{:S(2)}, u32[]{:S(2)}) %collective-permute-start.6) | collective-permute-done | bytes 589856 | tf_op jit(solution)/shard_map/ppermute | solution.py:11
  74.4 8.5 %convolution_convert_fusion.2 = bf16[2048,1152]{1,0:T(8,128)(2,1)} fusion(bf16[2048,1152]{1,0:T(8,128)(2,1)S(1)} %bitcast.61, bf16[1152,1152]{1,0:T(8,128)(2,1)S(1)} %pad_dynamic-update-slice_fusion.8), kind=kOutput, calls=%fused_computation.4 | convolution fusion | flops 5438177280 | bytes 12091392 | tf_op jit(solution)/shard_map/dot_general | solution.py:83
  83.0 8.3 %pad_maximum_fusion = bf16[2,16,128,1152]{3,2,1,0:T(8,128)(2,1)} fusion(bf16[1,16,128,1152]{3,2,1,0:T(8,128)(2,1)} %bitcast.60), kind=kLoop, calls=%fused_computation.2 | loop fusion | flops 4718592 | bytes 14155776 | tf_op jit(solution)/shard_map/stack | solution.py:86
  91.3 7.3 %all-to-all-start = ((bf16[2,16,128,1152]{3,2,1,0:T(8,128)(2,1)}), bf16[2,16,128,1152]{3,2,1,0:T(8,128)(2,1)}, u32[]{:S(2)}, u32[]{:S(2)}) async-start(bf16[2,16,128,1152]{3,2,1,0:T(8,128)(2,1)} %pad_maximum_fusion), calls=%async_computation | async-start | bytes 18874368 | tf_op jit(solution)/shard_map/all_to_all | solution.py:86
  98.7 0.8 pad_dynamic-update-slice_fusion.2
  99.5 0.7 pad_dynamic-update-slice_fusion.1
  100.9 10.9 %convolution_convert_fusion.1 = bf16[2048,1152]{1,0:T(8,128)(2,1)} fusion(bf16[2048,1152]{1,0:T(8,128)(2,1)} %bitcast.62, bf16[1152,1152]{1,0:T(8,128)(2,1)} %pad_dynamic-update-slice_fusion), kind=kOutput, calls=%fused_computation.3 | convolution fusion | flops 5438177280 | bytes 12091392 | tf_op jit(solution)/shard_map/dot_general | solution.py:81
  111.8 5.2 %reshape.77 = bf16[16,147456]{1,0:T(8,128)(2,1)} reshape(bf16[2048,1152]{1,0:T(8,128)(2,1)} %convolution_convert_fusion.1) | data formatting | bytes 9437184 | tf_op jit(solution)/shard_map/reshape | solution.py:82
  117.0 80.1 %all-to-all-done = bf16[2,16,128,1152]{3,2,1,0:T(8,128)(2,1)} async-done(((bf16[2,16,128,1152]{3,2,1,0:T(8,128)(2,1)}), bf16[2,16,128,1152]{3,2,1,0:T(8,128)(2,1)}, u32[]{:S(2)}, u32[]{:S(2)}) %all-to-all-start) | async-done | bytes 9437216 | tf_op jit(solution)/shard_map/all_to_all | solution.py:86
  197.1 12.7 %copy.10 = bf16[4,8,128,1152]{3,1,2,0:T(8,128)(2,1)} copy(bf16[4,8,128,1152]{3,2,1,0:T(8,128)(2,1)} %bitcast.24) | data formatting | bytes 18874368
  209.8 7.2 %fusion = bf16[16,147456]{1,0:T(8,128)(2,1)} fusion(bf16[16,32]{1,0:T(8,128)(2,1)S(1)} %copy-done, bf16[32,147456]{1,0:T(8,128)(2,1)} %bitcast.56), kind=kOutput, calls=%fused_computation.1 | convolution fusion | flops 153354240 | bytes 14156800 | tf_op jit(solution)/shard_map/dot_general | solution.py:94
  217.0 5.3 %reshape.75 = bf16[2048,1152]{1,0:T(8,128)(2,1)} reshape(bf16[16,147456]{1,0:T(8,128)(2,1)} %fusion) | data formatting | bytes 9437184 | tf_op jit(solution)/shard_map/reshape | solution.py:99
  222.3 12.6 %fusion.17 = (bf16[1152,1152]{1,0:T(8,128)(2,1)S(1)}, f32[1152,1152]{1,0:T(8,128)}) fusion(bf16[2048,1152]{1,0:T(8,128)(2,1)} %bitcast.63, bf16[2048,1152]{1,0:T(8,128)(2,1)} %reshape.75), kind=kOutput, calls=%fused_computation.68 | convolution fusion | flops 5437145088 | bytes 17399808 | tf_op jit(solution)/shard_map/dot_general | solution.py:100
  235.0 8.5 %collective-permute-start.11 = (bf16[128,1152]{1,0:T(8,128)(2,1)S(1)}, bf16[128,1152]{1,0:T(8,128)(2,1)S(1)}, u32[]{:S(2)}, u32[]{:S(2)}) collective-permute-start(bf16[128,1152]{1,0:T(8,128)(2,1)S(1)} %concatenate.90), channel_id=1, source_target_pairs={{2,0},{4,2},{6,4},{8,6},{10,8},{12,10},{14,12},{16,14},{18,16},{20... | collective-permute-start | bytes 884744 | tf_op jit(solution)/shard_map/ppermute | solution.py:11
  243.5 3.8 %collective-permute-start.12 = (bf16[128,1152]{1,0:T(8,128)(2,1)S(1)}, bf16[128,1152]{1,0:T(8,128)(2,1)S(1)}, u32[]{:S(2)}, u32[]{:S(2)}) collective-permute-start(bf16[128,1152]{1,0:T(8,128)(2,1)S(1)} %concatenate.91), channel_id=1, source_target_pairs={{0,2},{2,4},{4,6},{6,8},{8,10},{10,12},{12,14},{14,16},{16,18},{18... | collective-permute-start | bytes 884744 | tf_op jit(solution)/shard_map/ppermute | solution.py:11
  247.3 1.3 collective-permute-start.10
  249.4 4.3 %collective-permute-start.13 = (bf16[128,1152]{1,0:T(8,128)(2,1)}, bf16[128,1152]{1,0:T(8,128)(2,1)S(1)}, u32[]{:S(2)}, u32[]{:S(2)}) collective-permute-start(bf16[128,1152]{1,0:T(8,128)(2,1)} %concatenate.92), channel_id=1, source_target_pairs={{0,4},{2,6},{4,8},{6,10},{8,12},{10,14},{12,16},{14,18},{16,20},{1... | collective-permute-start | bytes 884744 | tf_op jit(solution)/shard_map/ppermute | solution.py:11
  254.5 4.7 %collective-permute-start.14 = (bf16[128,1152]{1,0:T(8,128)(2,1)}, bf16[128,1152]{1,0:T(8,128)(2,1)S(1)}, u32[]{:S(2)}, u32[]{:S(2)}) collective-permute-start(bf16[128,1152]{1,0:T(8,128)(2,1)} %concatenate.93), channel_id=1, source_target_pairs={{0,6},{2,8},{4,10},{6,12},{8,14},{10,16},{12,18},{14,20},{16,22},{... | collective-permute-start | bytes 884744 | tf_op jit(solution)/shard_map/ppermute | solution.py:11
  259.2 0.7 concatenate.88
  260.0 0.7 concatenate.94
  260.7 0.7 concatenate.87
  261.5 1.3 collective-permute-start.9
  262.8 4.3 %collective-permute-start.15 = (bf16[128,1152]{1,0:T(8,128)(2,1)}, bf16[128,1152]{1,0:T(8,128)(2,1)S(1)}, u32[]{:S(2)}, u32[]{:S(2)}) collective-permute-start(bf16[128,1152]{1,0:T(8,128)(2,1)} %concatenate.94), channel_id=1, source_target_pairs={{0,8},{2,10},{4,12},{6,14},{8,16},{10,18},{12,20},{14,22},{16,24},... | collective-permute-start | bytes 884744 | tf_op jit(solution)/shard_map/ppermute | solution.py:11
  267.1 1.3 collective-permute-start.8
  268.4 4.3 %fusion.18 = f32[16,32]{1,0:T(8,128)S(1)} fusion(bf16[16,147456]{1,0:T(8,128)(2,1)} %reshape.77, bf16[32,147456]{1,0:T(8,128)(2,1)S(1)} %bitcast.59), kind=kOutput, calls=%fused_computation.69 | convolution fusion | flops 150994944 | bytes 14157824 | tf_op jit(solution)/shard_map/dot_general | solution.py:90
  272.8 0.9 reshape.78
  273.7 19.4 %all-to-all-start.2 = ((f32[64,1,512]{2,1,0:T(1,128)}), f32[64,1,512]{2,1,0:T(1,128)S(1)}, u32[]{:S(2)}, u32[]{:S(2)}) async-start(f32[64,1,512]{2,1,0:T(1,128)} %reshape.78), calls=%async_computation.2 | async-start | bytes 262144 | tf_op jit(solution)/shard_map/all_to_all | solution.py:16
  293.2 2.2 fusion.7
  295.4 7.7 %all-to-all-done.2 = f32[64,1,512]{2,1,0:T(1,128)S(1)} async-done(((f32[64,1,512]{2,1,0:T(1,128)}), f32[64,1,512]{2,1,0:T(1,128)S(1)}, u32[]{:S(2)}, u32[]{:S(2)}) %all-to-all-start.2) | async-done | bytes 131104 | tf_op jit(solution)/shard_map/all_to_all | solution.py:16
  303.2 3.5 %all-to-all-start.1 = ((f32[2,64,1152]{2,1,0:T(8,128)}), f32[2,64,1152]{2,1,0:T(8,128)S(1)}, u32[]{:S(2)}, u32[]{:S(2)}) async-start(f32[2,64,1152]{2,1,0:T(8,128)} %bitcast.14), calls=%async_computation.1 | async-start | bytes 1179648 | tf_op jit(solution)/shard_map/all_to_all | solution.py:33
  307.2 1.0 reduce
  309.0 6.0 %all-to-all-done.1 = f32[2,64,1152]{2,1,0:T(8,128)S(1)} async-done(((f32[2,64,1152]{2,1,0:T(8,128)}), f32[2,64,1152]{2,1,0:T(8,128)S(1)}, u32[]{:S(2)}, u32[]{:S(2)}) %all-to-all-start.1) | async-done | bytes 589856 | tf_op jit(solution)/shard_map/all_to_all | solution.py:33
  315.1 0.7 select_multiply_fusion
  (88 shorter events, 7.4 us)
Async XLA Ops:
  0.6 209.2 %copy-start = (bf16[16,32]{1,0:T(8,128)(2,1)S(1)}, bf16[16,32]{1,0:T(8,128)(2,1)}, u32[]{:S(2)}) copy-start(bf16[16,32]{1,0:T(8,128)(2,1)} %param.9) | copy-start | bytes 3076
  4.7 22.1 %collective-permute-start = (bf16[2,128,1152]{2,1,0:T(8,128)(2,1)S(1)}, bf16[2,128,1152]{2,1,0:T(8,128)(2,1)S(1)}, u32[]{:S(2)}, u32[]{:S(2)}) collective-permute-start(bf16[2,128,1152]{2,1,0:T(8,128)(2,1)S(1)} %pad_maximum_fusion.1), channel_id=1, source_target_pairs={{0,8},{2,10},{4,12},{6,14},{8,16},{10,18},{12,20},{14,22},{16,24},... | collective-permute-start | bytes 1769480 | tf_op jit(solution)/shard_map/ppermute | solution.py:11
  10.4 24.6 %collective-permute-start.1 = (bf16[2,128,1152]{2,1,0:T(8,128)(2,1)S(1)}, bf16[2,128,1152]{2,1,0:T(8,128)(2,1)S(1)}, u32[]{:S(2)}, u32[]{:S(2)}) collective-permute-start(bf16[2,128,1152]{2,1,0:T(8,128)(2,1)S(1)} %pad_maximum_fusion.1), channel_id=1, source_target_pairs={{0,6},{2,8},{4,10},{6,12},{8,14},{10,16},{12,18},{14,20},{16,22},{... | collective-permute-start | bytes 1769480 | tf_op jit(solution)/shard_map/ppermute | solution.py:11
  15.7 32.0 %collective-permute-start.2 = (bf16[2,128,1152]{2,1,0:T(8,128)(2,1)S(1)}, bf16[2,128,1152]{2,1,0:T(8,128)(2,1)S(1)}, u32[]{:S(2)}, u32[]{:S(2)}) collective-permute-start(bf16[2,128,1152]{2,1,0:T(8,128)(2,1)S(1)} %pad_maximum_fusion.1), channel_id=1, source_target_pairs={{0,4},{2,6},{4,8},{6,10},{8,12},{10,14},{12,16},{14,18},{16,20},{1... | collective-permute-start | bytes 1769480 | tf_op jit(solution)/shard_map/ppermute | solution.py:11
  18.9 38.9 %collective-permute-start.3 = (bf16[2,128,1152]{2,1,0:T(8,128)(2,1)S(1)}, bf16[2,128,1152]{2,1,0:T(8,128)(2,1)S(1)}, u32[]{:S(2)}, u32[]{:S(2)}) collective-permute-start(bf16[2,128,1152]{2,1,0:T(8,128)(2,1)S(1)} %pad_maximum_fusion.1), channel_id=1, source_target_pairs={{0,2},{2,4},{4,6},{6,8},{8,10},{10,12},{12,14},{14,16},{16,18},{18... | collective-permute-start | bytes 1769480 | tf_op jit(solution)/shard_map/ppermute | solution.py:11
  20.8 37.0 %collective-permute-start.4 = (bf16[2,128,1152]{2,1,0:T(8,128)(2,1)S(1)}, bf16[2,128,1152]{2,1,0:T(8,128)(2,1)S(1)}, u32[]{:S(2)}, u32[]{:S(2)}) collective-permute-start(bf16[2,128,1152]{2,1,0:T(8,128)(2,1)S(1)} %pad_maximum_fusion.1), channel_id=1, source_target_pairs={{2,0},{4,2},{6,4},{8,6},{10,8},{12,10},{14,12},{16,14},{18,16},{20... | collective-permute-start | bytes 1769480 | tf_op jit(solution)/shard_map/ppermute | solution.py:11
  26.8 47.6 %copy-start.1 = (bf16[16,128,1152]{2,1,0:T(8,128)(2,1)}, bf16[16,128,1152]{2,1,0:T(8,128)(2,1)S(1)}, u32[]{:S(2)}) copy-start(bf16[16,128,1152]{2,1,0:T(8,128)(2,1)S(1)} %broadcast_select_fusion) | copy-start | bytes 14155780
  26.9 31.0 %collective-permute-start.5 = (bf16[2,128,1152]{2,1,0:T(8,128)(2,1)S(1)}, bf16[2,128,1152]{2,1,0:T(8,128)(2,1)S(1)}, u32[]{:S(2)}, u32[]{:S(2)}) collective-permute-start(bf16[2,128,1152]{2,1,0:T(8,128)(2,1)S(1)} %pad_maximum_fusion.1), channel_id=1, source_target_pairs={{4,0},{6,2},{8,4},{10,6},{12,8},{14,10},{16,12},{18,14},{20,16},{2... | collective-permute-start | bytes 1769480 | tf_op jit(solution)/shard_map/ppermute | solution.py:11
  35.0 37.6 %collective-permute-start.6 = (bf16[2,128,1152]{2,1,0:T(8,128)(2,1)S(1)}, bf16[2,128,1152]{2,1,0:T(8,128)(2,1)S(1)}, u32[]{:S(2)}, u32[]{:S(2)}) collective-permute-start(bf16[2,128,1152]{2,1,0:T(8,128)(2,1)S(1)} %pad_maximum_fusion.1), channel_id=1, source_target_pairs={{6,0},{8,2},{10,4},{12,6},{14,8},{16,10},{18,12},{20,14},{22,16},{... | collective-permute-start | bytes 1769480 | tf_op jit(solution)/shard_map/ppermute | solution.py:11
  47.7 25.4 %collective-permute-start.7 = (bf16[2,128,1152]{2,1,0:T(8,128)(2,1)S(1)}, bf16[2,128,1152]{2,1,0:T(8,128)(2,1)S(1)}, u32[]{:S(2)}, u32[]{:S(2)}) collective-permute-start(bf16[2,128,1152]{2,1,0:T(8,128)(2,1)S(1)} %pad_maximum_fusion.1), channel_id=1, source_target_pairs={{8,0},{10,2},{12,4},{14,6},{16,8},{18,10},{20,12},{22,14},{24,16},... | collective-permute-start | bytes 1769480 | tf_op jit(solution)/shard_map/ppermute | solution.py:11
  73.0 1.0 copy-start.2
  73.0 1.0 copy-start.3
  74.3 8.7 %copy-start.4 = (bf16[1152,1152]{1,0:T(8,128)(2,1)}, bf16[1152,1152]{1,0:T(8,128)(2,1)S(1)}, u32[]{:S(2)}) copy-start(bf16[1152,1152]{1,0:T(8,128)(2,1)S(1)} %get-tuple-element.32) | copy-start | bytes 7962628
  91.3 105.8 %all-to-all-start = ((bf16[2,16,128,1152]{3,2,1,0:T(8,128)(2,1)}), bf16[2,16,128,1152]{3,2,1,0:T(8,128)(2,1)}, u32[]{:S(2)}, u32[]{:S(2)}) async-start(bf16[2,16,128,1152]{3,2,1,0:T(8,128)(2,1)} %pad_maximum_fusion), calls=%async_computation | async-start | bytes 18874368 | tf_op jit(solution)/shard_map/all_to_all | solution.py:86
  217.0 51.4 %slice-start = ((s8[9437184]{0:T(1024)(128)(4,1)}), s8[1048576]{0:T(1024)(128)(4,1)S(1)}, s32[]{:S(2)}) async-start(s8[9437184]{0:T(1024)(128)(4,1)} %bitcast.57), calls=%async_computation.3 | async-start | bytes 2097152
  222.3 46.1 %slice-start.1 = ((s8[9437184]{0:T(1024)(128)(4,1)}), s8[4194304]{0:T(1024)(128)(4,1)S(1)}, s32[]{:S(2)}) async-start(s8[9437184]{0:T(1024)(128)(4,1)} %bitcast.57), calls=%async_computation.4 | async-start | bytes 8388608
  222.3 46.1 %slice-start.2 = ((s8[9437184]{0:T(1024)(128)(4,1)}), s8[4194304]{0:T(1024)(128)(4,1)S(1)}, s32[]{:S(2)}) async-start(s8[9437184]{0:T(1024)(128)(4,1)} %bitcast.57), calls=%async_computation.5 | async-start | bytes 8388608
  235.0 26.4 %collective-permute-start.11 = (bf16[128,1152]{1,0:T(8,128)(2,1)S(1)}, bf16[128,1152]{1,0:T(8,128)(2,1)S(1)}, u32[]{:S(2)}, u32[]{:S(2)}) collective-permute-start(bf16[128,1152]{1,0:T(8,128)(2,1)S(1)} %concatenate.90), channel_id=1, source_target_pairs={{2,0},{4,2},{6,4},{8,6},{10,8},{12,10},{14,12},{16,14},{18,16},{20... | collective-permute-start | bytes 884744 | tf_op jit(solution)/shard_map/ppermute | solution.py:11
  243.5 19.2 %collective-permute-start.12 = (bf16[128,1152]{1,0:T(8,128)(2,1)S(1)}, bf16[128,1152]{1,0:T(8,128)(2,1)S(1)}, u32[]{:S(2)}, u32[]{:S(2)}) collective-permute-start(bf16[128,1152]{1,0:T(8,128)(2,1)S(1)} %concatenate.91), channel_id=1, source_target_pairs={{0,2},{2,4},{4,6},{6,8},{8,10},{10,12},{12,14},{14,16},{16,18},{18... | collective-permute-start | bytes 884744 | tf_op jit(solution)/shard_map/ppermute | solution.py:11
  247.3 19.7 %collective-permute-start.10 = (bf16[128,1152]{1,0:T(8,128)(2,1)S(1)}, bf16[128,1152]{1,0:T(8,128)(2,1)S(1)}, u32[]{:S(2)}, u32[]{:S(2)}) collective-permute-start(bf16[128,1152]{1,0:T(8,128)(2,1)S(1)} %concatenate.89), channel_id=1, source_target_pairs={{4,0},{6,2},{8,4},{10,6},{12,8},{14,10},{16,12},{18,14},{20,16},{2... | collective-permute-start | bytes 884744 | tf_op jit(solution)/shard_map/ppermute | solution.py:11
  249.4 43.8 %collective-permute-start.13 = (bf16[128,1152]{1,0:T(8,128)(2,1)}, bf16[128,1152]{1,0:T(8,128)(2,1)S(1)}, u32[]{:S(2)}, u32[]{:S(2)}) collective-permute-start(bf16[128,1152]{1,0:T(8,128)(2,1)} %concatenate.92), channel_id=1, source_target_pairs={{0,4},{2,6},{4,8},{6,10},{8,12},{10,14},{12,16},{14,18},{16,20},{1... | collective-permute-start | bytes 884744 | tf_op jit(solution)/shard_map/ppermute | solution.py:11
  254.5 38.7 %collective-permute-start.14 = (bf16[128,1152]{1,0:T(8,128)(2,1)}, bf16[128,1152]{1,0:T(8,128)(2,1)S(1)}, u32[]{:S(2)}, u32[]{:S(2)}) collective-permute-start(bf16[128,1152]{1,0:T(8,128)(2,1)} %concatenate.93), channel_id=1, source_target_pairs={{0,6},{2,8},{4,10},{6,12},{8,14},{10,16},{12,18},{14,20},{16,22},{... | collective-permute-start | bytes 884744 | tf_op jit(solution)/shard_map/ppermute | solution.py:11
  261.5 31.7 %collective-permute-start.9 = (bf16[128,1152]{1,0:T(8,128)(2,1)}, bf16[128,1152]{1,0:T(8,128)(2,1)S(1)}, u32[]{:S(2)}, u32[]{:S(2)}) collective-permute-start(bf16[128,1152]{1,0:T(8,128)(2,1)} %concatenate.88), channel_id=1, source_target_pairs={{6,0},{8,2},{10,4},{12,6},{14,8},{16,10},{18,12},{20,14},{22,16},{... | collective-permute-start | bytes 884744 | tf_op jit(solution)/shard_map/ppermute | solution.py:11
  262.8 30.4 %collective-permute-start.15 = (bf16[128,1152]{1,0:T(8,128)(2,1)}, bf16[128,1152]{1,0:T(8,128)(2,1)S(1)}, u32[]{:S(2)}, u32[]{:S(2)}) collective-permute-start(bf16[128,1152]{1,0:T(8,128)(2,1)} %concatenate.94), channel_id=1, source_target_pairs={{0,8},{2,10},{4,12},{6,14},{8,16},{10,18},{12,20},{14,22},{16,24},... | collective-permute-start | bytes 884744 | tf_op jit(solution)/shard_map/ppermute | solution.py:11
  267.1 26.1 %collective-permute-start.8 = (bf16[128,1152]{1,0:T(8,128)(2,1)}, bf16[128,1152]{1,0:T(8,128)(2,1)S(1)}, u32[]{:S(2)}, u32[]{:S(2)}) collective-permute-start(bf16[128,1152]{1,0:T(8,128)(2,1)} %concatenate.87), channel_id=1, source_target_pairs={{8,0},{10,2},{12,4},{14,6},{16,8},{18,10},{20,12},{22,14},{24,16},... | collective-permute-start | bytes 884744 | tf_op jit(solution)/shard_map/ppermute | solution.py:11
  273.7 29.4 %all-to-all-start.2 = ((f32[64,1,512]{2,1,0:T(1,128)}), f32[64,1,512]{2,1,0:T(1,128)S(1)}, u32[]{:S(2)}, u32[]{:S(2)}) async-start(f32[64,1,512]{2,1,0:T(1,128)} %reshape.78), calls=%async_computation.2 | async-start | bytes 262144 | tf_op jit(solution)/shard_map/all_to_all | solution.py:16
  303.2 11.9 %all-to-all-start.1 = ((f32[2,64,1152]{2,1,0:T(8,128)}), f32[2,64,1152]{2,1,0:T(8,128)S(1)}, u32[]{:S(2)}, u32[]{:S(2)}) async-start(f32[2,64,1152]{2,1,0:T(8,128)} %bitcast.14), calls=%async_computation.1 | async-start | bytes 1179648 | tf_op jit(solution)/shard_map/all_to_all | solution.py:33
